TPU v7x, 128 devices: a whole 4x4x4 slice. The times are simulated.
128 devices in a mesh: blk: 64 (over z_lo, x, y, core), grp: 2 (over z_hi).
Axes of the slice: x: 4, y: 4, z: 4 (z_hi: 2, z_lo: 2; z = z_hi * 2 + z_lo), core: 2. Of those that a mesh axis runs over, the one named last changes fastest.
Arguments:
- returns: float32 [512, 32768], P(None, ('blk', 'grp')), may hold values from -200 to 200
Outputs:
- correlation: bfloat16 [32768, 32768], P(('blk', 'grp'))
All inputs are finite; a program needn't handle non-finite values.
Results may differ from a plain program's by a relative error of at most 0.0034.
Values may be sent and summed in bfloat16 or wider, within the bound.
A program may use at most 128 MiB of HBM per device.

v0:
```python
import math
import jax
import jax.numpy as jnp
from jax import lax
from jax.sharding import Mesh
from jax.sharding import PartitionSpec as P

BLK_GRP = ("blk_0", "blk_1", "blk_2", "blk_3", "grp")


def by_axis(array, axes):
    for axis in axes:
        array = lax.psum(array, axis)
    return array


def gram_tile(first, second):
    return lax.dot_general(
        first, second, (((0,), (0,)), ((), ())), preferred_element_type=jnp.float32
    )


def shards(returns):
    bar_count = returns.shape[0]
    series_dev = returns.shape[1]
    devices = lax.axis_size(BLK_GRP)
    my_index = lax.axis_index(BLK_GRP)
    summed = by_axis(jnp.sum(returns, axis=1), BLK_GRP)
    market = summed / (series_dev * devices)
    excess = returns - market[:, None]
    deviation = excess - jnp.mean(excess, axis=0, keepdims=True)
    inverse = lax.rsqrt(jnp.mean(deviation * deviation, axis=0, keepdims=True) + 1e-06) / math.sqrt(
        bar_count
    )
    zscores = (deviation * inverse).astype(jnp.bfloat16)
    piece = lax.all_gather(zscores, BLK_GRP, axis=1, tiled=True)
    products = gram_tile(zscores, piece)
    column_block = jnp.arange(piece.shape[1], dtype=jnp.int32) // series_dev
    return jnp.where(column_block[None, :] >= my_index, products, jnp.float32(0.0)).astype(
        jnp.bfloat16
    )


def solution(mesh):
    split = Mesh(
        mesh.devices.reshape(2, 4, 4, 2, mesh.shape["grp"]),
        ("blk_0", "blk_1", "blk_2", "blk_3", "grp"),
    )
    in_specs = (P(None, BLK_GRP),)
    out_specs = P(BLK_GRP, None)
    return jax.shard_map(
        shards, mesh=split, in_specs=in_specs, out_specs=out_specs, check_vma=False
    )
```

profile of v0, /device:TPU:1, one launch (start us, length us, event | category | flops | bytes accessed | tf_op | source)
XLA Modules:
  0.0 429.9 jit_solution(4869989052520204716)
XLA Ops:
  6.5 0.0 all-gather.2.cloned.1.call-start
  6.5 1.2 reduce_sum.27
  7.7 4.8 %psum.35 = f32[512]{0:T(512)S(1)} all-reduce(f32[512]{0:T(512)S(1)} %reduce_sum.27), channel_id=1, replica_groups=mesh['blk_0'=2,'blk_1'=4,'blk_2'=4,'blk_3'=2,'grp'=2] {'blk_0'}, use_global_device_ids=true, to_apply=%region_1.0 | all-reduce | flops 512 | bytes 4096 | tf_op jit(solution)/shard_map/psum | solution.py:13
  12.5 8.4 %psum.36 = f32[512]{0:T(512)S(1)} all-reduce(f32[512]{0:T(512)S(1)} %psum.35), channel_id=1, replica_groups=mesh['blk_0'=2,'blk_1'=4,'blk_2'=4,'blk_3'=2,'grp'=2] {'blk_1'}, use_global_device_ids=true, to_apply=%region_2.0 | all-reduce | flops 512 | bytes 4096 | tf_op jit(solution)/shard_map/psum | solution.py:13
  20.9 8.7 %psum.37 = f32[512]{0:T(512)S(1)} all-reduce(f32[512]{0:T(512)S(1)} %psum.36), channel_id=1, replica_groups=mesh['blk_0'=2,'blk_1'=4,'blk_2'=4,'blk_3'=2,'grp'=2] {'blk_2'}, use_global_device_ids=true, to_apply=%region_3.0 | all-reduce | flops 512 | bytes 4096 | tf_op jit(solution)/shard_map/psum | solution.py:13
  29.6 7.8 %psum.38 = f32[512]{0:T(512)S(1)} all-reduce(f32[512]{0:T(512)S(1)} %psum.37), channel_id=1, replica_groups=mesh['blk_0'=2,'blk_1'=4,'blk_2'=4,'blk_3'=2,'grp'=2] {'blk_3'}, use_global_device_ids=true, to_apply=%region_4.0 | all-reduce | flops 512 | bytes 4096 | tf_op jit(solution)/shard_map/psum | solution.py:13
  37.4 5.9 %psum.39 = f32[512]{0:T(512)S(1)} all-reduce(f32[512]{0:T(512)S(1)} %psum.38), channel_id=1, replica_groups=mesh['blk_0'=2,'blk_1'=4,'blk_2'=4,'blk_3'=2,'grp'=2] {'grp'}, use_global_device_ids=true, to_apply=%region_5.0 | all-reduce | flops 512 | bytes 4096 | tf_op jit(solution)/shard_map/psum | solution.py:13
  43.3 1.2 subtract_reduce_fusion
  44.5 1.2 multiply_reduce_fusion
  45.7 1.9 multiply_convert_fusion
  47.6 0.0 all-gather.2.cloned.1.call-update
  47.7 354.2 %all-gather.2.cloned.1.call-done = bf16[512,32768]{1,0:T(8,128)(2,1)} async-done(((bf16[512,256]{1,0:T(8,128)(2,1)}), bf16[512,32768]{1,0:T(8,128)(2,1)}) %all-gather.2.cloned.1.call-update) | async-done | bytes 33554448 | tf_op jit(solution)/shard_map/all_gather | solution.py:36
  401.9 21.2 %fusion = bf16[256,32768]{1,0:T(8,128)(2,1)} fusion(bf16[512,256]{1,0:T(8,128)(2,1)} %multiply_convert_fusion, bf16[512,32768]{1,0:T(8,128)(2,1)} %all-gather.2.cloned.1.call-done, pred[32768]{0:T(1024)(128)(4,1)S(1)} %fusion.1), kind=kOutput, calls=%fused_computation.1 | convolution fusion | flops 8606711808 | bytes 50626560 | tf_op jit(solution)/shard_map/dot_general | solution.py:18
  (4 shorter events, 0.1 us)
Async XLA Ops:
  6.5 395.3 %all-gather.2.cloned.1.call-start = ((), (), s32[]{:S(2)}) async-start(), calls=%async_computation | async-start | bytes 33816576 | tf_op jit(solution)/shard_map/all_gather | solution.py:36
Sparse Core Ops, SparseCore 0:
  47.8 354.0 all-gather.1
where the time goes:
time: 430 us
  waiting for transfers between devices  354 us (82%)
  blocking collectives  35.6 us (8%)
  matrix products  21.2 us (5%)
  between operations  13.4 us (3%)
  other arithmetic  5.51 us (1%)
    all_gather x1, waiting for transfers between devices, shards(): piece = lax.all_gather(zscores, BLK_GRP, axis=1, tiled=True)  354 us
    psum x5, blocking collectives, by_axis(): array = lax.psum(array, axis)  35.6 us
    dot_general x1, matrix products, gram_tile(): lax.dot_general(first, second, (((0,), (0,)), ((), ())), preferred_elemen...  21.2 us
  transfers between devices with their start and end apart: 1, of which 1 were waited for; matrix products, arithmetic and copies ran while one was open for 0% of the time, Pallas kernels for 0%

commit v1 on v0

--- a/solution.py
+++ b/solution.py
@@ -33,7 +33,10 @@
         bar_count
     )
     zscores = (deviation * inverse).astype(jnp.bfloat16)
-    piece = lax.all_gather(zscores, BLK_GRP, axis=1, tiled=True)
+    size = lax.axis_size(BLK_GRP)
+    blocks = jnp.stack([zscores for _ in range(size)])
+    blocks = lax.all_to_all(blocks, BLK_GRP, split_axis=0, concat_axis=0)
+    piece = jnp.concatenate(blocks, axis=1)
     products = gram_tile(zscores, piece)
     column_block = jnp.arange(piece.shape[1], dtype=jnp.int32) // series_dev
     return jnp.where(column_block[None, :] >= my_index, products, jnp.float32(0.0)).astype(

time: 430 us -> 608 us (1.41)
  the two profiles are of different devices: /device:TPU:1 before, /device:TPU:5 now
where the time goes in v1:
time: 608 us; the launch traced here: 607 us
  waiting for transfers between devices  530 us (87%)
  blocking collectives  32.6 us (5%)
  matrix products  19.1 us (3%)
  local copies, waits for them, and re-layouts  11.2 us (2%)
  starting transfers between devices  9.11 us (1%)
    all_to_all x1, waiting for transfers between devices, shards(): blocks = lax.all_to_all(blocks, BLK_GRP, split_axis=0, concat_axis=0)  530 us
    psum x5, blocking collectives, by_axis(): array = lax.psum(array, axis)  32.6 us
    dot_general x1, matrix products, gram_tile(): lax.dot_general(first, second, (((0,), (0,)), ((), ())), preferred_elemen...  19.1 us
  transfers between devices with their start and end apart: 1, of which 1 were waited for; matrix products, arithmetic and copies ran while one was open for 0% of the time, Pallas kernels for 0%

profile of v1, /device:TPU:5, one launch (start us, length us, event | category | flops | bytes accessed | tf_op | source)
XLA Modules:
  0.0 607.1 jit_solution(6196766640221029567)
XLA Ops:
  0.0 1.2 reduce_sum.27
  1.2 4.0 psum.35
  5.1 6.3 %psum.36 = f32[512]{0:T(512)S(1)} all-reduce(f32[512]{0:T(512)S(1)} %psum.35), channel_id=1, replica_groups=mesh['blk_0'=2,'blk_1'=4,'blk_2'=4,'blk_3'=2,'grp'=2] {'blk_1'}, use_global_device_ids=true, to_apply=%region_2.0 | all-reduce | flops 512 | bytes 4096 | tf_op jit(solution)/shard_map/psum | solution.py:13
  11.4 8.7 %psum.37 = f32[512]{0:T(512)S(1)} all-reduce(f32[512]{0:T(512)S(1)} %psum.36), channel_id=1, replica_groups=mesh['blk_0'=2,'blk_1'=4,'blk_2'=4,'blk_3'=2,'grp'=2] {'blk_2'}, use_global_device_ids=true, to_apply=%region_3.0 | all-reduce | flops 512 | bytes 4096 | tf_op jit(solution)/shard_map/psum | solution.py:13
  20.1 7.8 %psum.38 = f32[512]{0:T(512)S(1)} all-reduce(f32[512]{0:T(512)S(1)} %psum.37), channel_id=1, replica_groups=mesh['blk_0'=2,'blk_1'=4,'blk_2'=4,'blk_3'=2,'grp'=2] {'blk_3'}, use_global_device_ids=true, to_apply=%region_4.0 | all-reduce | flops 512 | bytes 4096 | tf_op jit(solution)/shard_map/psum | solution.py:13
  27.9 5.9 psum.39
  33.8 1.2 subtract_reduce_fusion
  35.0 1.2 multiply_reduce_fusion
  36.2 1.2 multiply_convert_fusion
  37.4 0.1 copy.2
  37.6 11.1 %stack.2 = bf16[128,512,256]{1,2,0:T(8,128)(2,1)} broadcast(bf16[512,256]{0,1:T(8,128)(2,1)S(1)} %copy.2), dimensions={1,2} | broadcast | bytes 33816576 | tf_op jit(solution)/shard_map/stack | solution.py:37
  48.6 9.1 %all-to-all-start = ((bf16[128,512,256]{1,2,0:T(8,128)(2,1)}), bf16[128,512,256]{1,2,0:T(8,128)(2,1)}, u32[]{:S(2)}, u32[]{:S(2)}) async-start(bf16[128,512,256]{1,2,0:T(8,128)(2,1)} %stack.2), calls=%async_computation | async-start | bytes 67108864 | tf_op jit(solution)/shard_map/all_to_all | solution.py:38
  57.8 530.3 %all-to-all-done = bf16[128,512,256]{1,2,0:T(8,128)(2,1)} async-done(((bf16[128,512,256]{1,2,0:T(8,128)(2,1)}), bf16[128,512,256]{1,2,0:T(8,128)(2,1)}, u32[]{:S(2)}, u32[]{:S(2)}) %all-to-all-start) | async-done | bytes 33554464 | tf_op jit(solution)/shard_map/all_to_all | solution.py:38
  588.0 19.1 %fusion = bf16[256,32768]{1,0:T(8,128)(2,1)} fusion(bf16[512,256]{1,0:T(8,128)(2,1)S(1)} %multiply_convert_fusion, bf16[512,32768]{0,1:T(8,128)(2,1)} %bitcast.1, pred[32768]{0:T(1024)(128)(4,1)S(1)} %fusion.1), kind=kOutput, calls=%fused_computation.1 | convolution fusion | flops 8606711808 | bytes 50626560 | tf_op jit(solution)/shard_map/dot_general | solution.py:18
  (4 shorter events, 0.1 us)
Async XLA Ops:
  48.6 539.4 %all-to-all-start = ((bf16[128,512,256]{1,2,0:T(8,128)(2,1)}), bf16[128,512,256]{1,2,0:T(8,128)(2,1)}, u32[]{:S(2)}, u32[]{:S(2)}) async-start(bf16[128,512,256]{1,2,0:T(8,128)(2,1)} %stack.2), calls=%async_computation | async-start | bytes 67108864 | tf_op jit(solution)/shard_map/all_to_all | solution.py:38
